TPU v7x, 128 devices: a whole 4x4x4 slice. The times are simulated.
128 devices in a mesh: row: 8 (over x, z_hi), col: 16 (over y, z_lo, core).
Axes of the slice: x: 4, y: 4, z: 4 (z_hi: 2, z_lo: 2; z = z_hi * 2 + z_lo), core: 2. Of those that a mesh axis runs over, the one named last changes fastest.
Arguments:
- gradients: bfloat16 [3, 128, 512, 512], P(None, None, ('row', 'col')), may hold values from -6 to 6
- factors: float32 [2, 128, 512, 512], P(None, None, ('row', 'col')), as said below
- slot_block: int32 [128], replicated, may hold values from 0 to 127, each once
- layer_of_block: int32 [128], replicated, may hold values from 0 to 3
- layer_step_scale: float32 [4], replicated, may hold values from 0.25 to 4
Outputs:
- new_factors: float32 [2, 128, 512, 512], P(None, ('row', 'col'))
- update: bfloat16 [128, 512, 512], P(None, ('row', 'col'))
Inputs may be any that keep to these rules, and one draw needn't show every extreme that they name: Every block factors[i, b] is symmetric positive definite with eigenvalues of 0.25 or more. `slot_block`: each block number stands in exactly one slot; slot j belongs to owner device j in the order of row+col (one slot per device).
All inputs are finite; a program needn't handle non-finite values.
Results may differ from a plain program's by a relative error of at most 0.0069.
Values may be sent and summed in bfloat16 or wider, within the bound.
No kernel may reach another device: no remote copies, remote signals or barrier semaphores. Data moves between devices by JAX's collectives and lax.ppermute only.
A program may use at most 64 MiB of HBM per device.

v0:
```python
import jax
import jax.numpy as jnp
from jax import lax
from jax.experimental import pallas as pl
from jax.experimental.pallas import tpu as pltpu
from jax.sharding import PartitionSpec as P

ITERS = 6
TILE = 128
BF = jnp.bfloat16
F32 = jnp.float32


def pack_body(slots, grads, factors, msg, fac_in, fac_out, sem_g, sem_f, sem_o):
    steps, blocks, rows, side = grads.shape
    wide = steps * side
    load = pltpu.make_async_copy(factors, fac_in, sem_f)
    load.start()

    def send(j, carry):
        block = slots[j]
        for s in range(steps):
            pltpu.make_async_copy(
                grads.at[s, block], msg.at[j, :, pl.ds(s * side, side)], sem_g
            ).start()
        return carry

    lax.fori_loop(0, blocks, send, 0, unroll=8)
    load.wait()
    band = lax.axis_index("row") // 2
    tiles = side // TILE
    starts = [pl.multiple_of(lax.rem(band + t, tiles) * TILE, TILE) for t in range(tiles - 1)]

    def convert(j, carry):
        block = slots[j]
        for f in range(2):
            for t in range(tiles - 1):
                piece = fac_in[f, block, :, pl.ds(starts[t], TILE)]
                fac_out[j, :, pl.ds((f * (tiles - 1) + t) * TILE, TILE)] = piece.astype(BF)
        return carry

    lax.fori_loop(0, blocks, convert, 0, unroll=8)
    narrow = fac_out.shape[2]
    store = pltpu.make_async_copy(fac_out, msg.at[:, :, pl.ds(wide, narrow)], sem_o)
    store.start()
    sent = msg.at[:, :, pl.ds(0, wide)]
    pltpu.make_async_copy(sent, sent, sem_g).wait()
    store.wait()


def pack(slots, grads, factors):
    steps, blocks, rows, side = grads.shape
    narrow = 2 * (side - TILE)
    return pl.pallas_call(
        pack_body,
        out_shape=jax.ShapeDtypeStruct((blocks, rows, steps * side + narrow), BF),
        in_specs=[
            pl.BlockSpec(memory_space=pltpu.SMEM),
            pl.BlockSpec(memory_space=pl.ANY),
            pl.BlockSpec(memory_space=pl.ANY),
        ],
        out_specs=pl.BlockSpec(memory_space=pl.ANY),
        scratch_shapes=[
            pltpu.VMEM(factors.shape, F32),
            pltpu.VMEM((blocks, rows, narrow), BF),
            pltpu.SemaphoreType.DMA,
            pltpu.SemaphoreType.DMA,
            pltpu.SemaphoreType.DMA,
        ],
    )(slots, grads, factors)


def mm(a, b):
    return jnp.dot(a, b, preferred_element_type=F32)


def step_of(m):
    mb = m.astype(BF)
    square = mm(mb, mb)
    w = (0.0625 * square - 0.625 * m).astype(BF)
    v = 1.5625 * m + mm(w, mb)
    return 1.5625 * v + mm(w, v.astype(BF))


def compute_body(slots, layers, scales, got, stats, update, stat_ref, m_ref, x_ref, g_ref, sem):
    sources, rows, _ = got.shape
    side = sources * rows
    tiles = side // TILE
    per = sources // tiles
    steps = g_ref.shape[0]
    grams = [None, None]
    for s in range(steps):
        g_ref[s] = got[:, :, s * side : (s + 1) * side].reshape(side, side)
    for s in range(steps):
        g = g_ref[s]
        gt = g.T
        left = mm(g, gt)
        right = mm(gt, g)
        grams = [left, right] if s == 0 else [grams[0] + left, grams[1] + right]
    for f in range(2):
        stat_ref[f, 0] = grams[f] / side
        for i in range(tiles):
            for t in range(tiles - 1):
                k = (i + t) % tiles
                lo = steps * side + (f * (tiles - 1) + t) * TILE
                held = got[i * per : (i + 1) * per, :, lo : lo + TILE]
                held = held.astype(F32).reshape(TILE, TILE)
                a = pl.ds(i * TILE, TILE)
                c = pl.ds(k * TILE, TILE)
                stat_ref[f, 0, a, c] += held
                if t == 1:
                    stat_ref[f, 0, c, a] += held.T
    out = pltpu.make_async_copy(stat_ref, stats, sem)
    out.start()
    eye = (
        lax.broadcasted_iota(jnp.int32, (side, side), 0)
        == lax.broadcasted_iota(jnp.int32, (side, side), 1)
    )
    for f in range(2):
        a = stat_ref[f, 0]
        total = jnp.sum(jnp.sum(a * a, axis=0, keepdims=True), axis=1, keepdims=True)
        norm = jnp.sqrt(total)
        first = lax.rsqrt(jnp.sqrt(norm))
        m = a * (1.0 / norm)
        x_ref[f] = first * (jnp.where(eye, 1.25, 0.0) - 0.25 * m)
        m_ref[f] = step_of(m)

    def sweep(k, carry):
        for f in range(2):
            m = m_ref[f]
            x = x_ref[f]
            x_ref[f] = 1.25 * x - 0.25 * mm(x.astype(BF), m.astype(BF))
            m_ref[f] = step_of(m)
        return carry

    lax.fori_loop(1, ITERS - 1, sweep, 0)
    roots = []
    for f in range(2):
        x = x_ref[f]
        roots.append((1.25 * x - 0.25 * mm(x.astype(BF), m_ref[f].astype(BF))).astype(BF))
    me = lax.axis_index("row") * lax.axis_size("col") + lax.axis_index("col")
    scale = scales[layers[slots[me]]]
    applied = mm(roots[0], g_ref[steps - 1]).astype(BF)
    result = (scale * mm(applied, roots[1])).astype(BF)
    update[...] = result.reshape(sources, rows, side)
    out.wait()


def compute(slots, layers, scales, got, steps):
    sources, rows, _ = got.shape
    side = sources * rows
    smem = pl.BlockSpec(memory_space=pltpu.SMEM)
    return pl.pallas_call(
        compute_body,
        out_shape=(
            jax.ShapeDtypeStruct((2, 1, side, side), F32),
            jax.ShapeDtypeStruct((sources, rows, side), BF),
        ),
        in_specs=[smem, smem, smem, pl.BlockSpec(memory_space=pltpu.VMEM)],
        out_specs=(
            pl.BlockSpec(memory_space=pl.ANY),
            pl.BlockSpec(memory_space=pltpu.VMEM),
        ),
        scratch_shapes=[
            pltpu.VMEM((2, 1, side, side), F32),
            pltpu.VMEM((2, side, side), F32),
            pltpu.VMEM((2, side, side), F32),
            pltpu.VMEM((steps, side, side), BF),
            pltpu.SemaphoreType.DMA,
        ],
    )(slots, layers, scales, got)


def unpack_body(slots, got, update, sem):
    blocks = got.shape[0]

    def place(j, carry):
        pltpu.make_async_copy(got.at[j], update.at[slots[j]], sem).start()
        return carry

    lax.fori_loop(0, blocks, place, 0, unroll=8)
    pltpu.make_async_copy(update, update, sem).wait()


def unpack(slots, got):
    return pl.pallas_call(
        unpack_body,
        out_shape=jax.ShapeDtypeStruct(got.shape, got.dtype),
        in_specs=[
            pl.BlockSpec(memory_space=pltpu.SMEM),
            pl.BlockSpec(memory_space=pl.ANY),
        ],
        out_specs=pl.BlockSpec(memory_space=pl.ANY),
        scratch_shapes=[pltpu.SemaphoreType.DMA],
    )(slots, got)


def body(gradients, factors, slot_block, layer_of_block, layer_step_scale):
    axes = ("row", "col")
    message = pack(slot_block, gradients, factors)
    owned = lax.all_to_all(message, axes, split_axis=0, concat_axis=0, tiled=True)
    new_factors, moved = compute(
        slot_block, layer_of_block, layer_step_scale, owned, gradients.shape[0]
    )
    returned = lax.all_to_all(moved, axes, split_axis=0, concat_axis=0, tiled=True)
    return (new_factors, unpack(slot_block, returned))


def solution(mesh):
    return jax.shard_map(
        body,
        mesh=mesh,
        in_specs=(
            P(None, None, ("row", "col"), None),
            P(None, None, ("row", "col"), None),
            P(),
            P(),
            P(),
        ),
        out_specs=(P(None, ("row", "col"), None, None), P(None, ("row", "col"), None)),
        check_vma=False,
    )
```

profile of v0, /device:TPU:1, one launch (start us, length us, event | category | flops | bytes accessed | tf_op | source)
XLA Modules:
  0.0 149.5 jit_solution(17427155691889620498)
XLA Ops:
  0.6 49.5 %shard_map.68 = bf16[128,4,2304]{2,1,0:T(4,128)(2,1)} custom-call(s32[128]{0:T(128)} %slots.5, bf16[3,128,4,512]{3,2,1,0:T(4,128)(2,1)} %grads.1, f32[2,128,4,512]{3,2,1,0:T(4,128)} %factors.1), custom_call_target="tpu_custom_call" | custom-call | tf_op jit(solution)/shard_map/pallas_call | solution.py:54
  50.1 44.1 %all_to_all.10.got = bf16[128,4,2304]{2,1,0:T(4,128)(2,1)} all-to-all(bf16[128,4,2304]{2,1,0:T(4,128)(2,1)} %shard_map.68), channel_id=1, replica_groups=mesh['row'=8,'col'=16] {'row','col'}, dimensions={0} | all-to-all | bytes 4718592 | tf_op jit(solution)/shard_map/all_to_all | solution.py:201
  94.3 17.7 %shard_map.69 = (f32[2,1,512,512]{3,2,1,0:T(8,128)}, bf16[128,4,512]{2,1,0:T(4,128)(2,1)}) custom-call(s32[128]{0:T(128)} %slots.5, s32[128]{0:T(128)} %layers.1, f32[4]{0:T(128)} %scales.1, bf16[128,4,2304]{2,1,0:T(4,128)(2,1)} %all_to_all.10.got), custom_call_target="tpu_custom_call" | custom-call | tf_op jit(solution)/shard_map/pallas_call | solution.py:153
  112.0 19.8 %all_to_all.11.got = bf16[128,4,512]{2,1,0:T(4,128)(2,1)} all-to-all(bf16[128,4,512]{2,1,0:T(4,128)(2,1)} %get-tuple-element.5), channel_id=1, replica_groups=mesh['row'=8,'col'=16] {'row','col'}, dimensions={0} | all-to-all | bytes 1048576 | tf_op jit(solution)/shard_map/all_to_all | solution.py:205
  131.8 17.7 %shard_map.70 = bf16[128,4,512]{2,1,0:T(4,128)(2,1)} custom-call(s32[128]{0:T(128)} %slots.5, bf16[128,4,512]{2,1,0:T(4,128)(2,1)} %all_to_all.11.got), custom_call_target="tpu_custom_call" | custom-call | tf_op jit(solution)/shard_map/pallas_call | solution.py:186
where the time goes:
time: 150 us; the launch traced here: 149 us
  Pallas kernels  84.9 us (57%)
  blocking collectives  63.9 us (43%)
    pallas_call x1, Pallas kernels, pack(): pl.pallas_call(pack_body, out_shape=jax.ShapeDtypeStruct((blocks, rows, s...  49.5 us
    all_to_all x1, blocking collectives, body(): lax.all_to_all(message, axes, split_axis=0, concat_axis=0, tiled=True)  44.1 us
    all_to_all x1, blocking collectives, body(): lax.all_to_all(moved, axes, split_axis=0, concat_axis=0, tiled=True)  19.8 us
    pallas_call x1, Pallas kernels, compute(): pl.pallas_call(compute_body, out_shape=(jax.ShapeDtypeStruct((2, 1, side,...  17.7 us
    pallas_call x1, Pallas kernels, unpack(): pl.pallas_call(unpack_body, out_shape=jax.ShapeDtypeStruct(got.shape, got...  17.7 us

commit v1 on v0

--- a/solution.py
+++ b/solution.py
@@ -11,49 +11,58 @@
 F32 = jnp.float32
 
 
-def pack_body(slots, grads, factors, msg, fac_in, fac_out, sem_g, sem_f, sem_o):
+def pack_body(slots, grads, factors, msg, g_in, f_in, out, sem_g, sem_f, sem_o):
     steps, blocks, rows, side = grads.shape
     wide = steps * side
-    load = pltpu.make_async_copy(factors, fac_in, sem_f)
-    load.start()
-
-    def send(j, carry):
-        block = slots[j]
-        for s in range(steps):
-            pltpu.make_async_copy(
-                grads.at[s, block], msg.at[j, :, pl.ds(s * side, side)], sem_g
-            ).start()
-        return carry
-
-    lax.fori_loop(0, blocks, send, 0, unroll=8)
-    load.wait()
+    tiles = side // TILE
+    narrow = (tiles - 1) * TILE
+    loads = [pltpu.make_async_copy(grads.at[s], g_in.at[s], sem_g.at[s]) for s in range(steps)]
+    loads += [pltpu.make_async_copy(factors.at[f], f_in.at[f], sem_f.at[f]) for f in range(2)]
+    for load in loads:
+        load.start()
+    stores = []
+
+    def flush(lo, size):
+        span = pl.ds(lo, size)
+        store = pltpu.make_async_copy(
+            out.at[:, :, span], msg.at[:, :, span], sem_o.at[len(stores)]
+        )
+        store.start()
+        stores.append(store)
+
+    for s in range(steps):
+        loads[s].wait()
+
+        def gather(j, carry):
+            out[j, :, pl.ds(s * side, side)] = g_in[s, slots[j]]
+            return carry
+
+        lax.fori_loop(0, blocks, gather, 0, unroll=16)
+        flush(s * side, side)
     band = lax.axis_index("row") // 2
-    tiles = side // TILE
     starts = [pl.multiple_of(lax.rem(band + t, tiles) * TILE, TILE) for t in range(tiles - 1)]
-
-    def convert(j, carry):
-        block = slots[j]
-        for f in range(2):
+    for f in range(2):
+        loads[steps + f].wait()
+
+        def convert(j, carry):
+            block = slots[j]
             for t in range(tiles - 1):
-                piece = fac_in[f, block, :, pl.ds(starts[t], TILE)]
-                fac_out[j, :, pl.ds((f * (tiles - 1) + t) * TILE, TILE)] = piece.astype(BF)
-        return carry
-
-    lax.fori_loop(0, blocks, convert, 0, unroll=8)
-    narrow = fac_out.shape[2]
-    store = pltpu.make_async_copy(fac_out, msg.at[:, :, pl.ds(wide, narrow)], sem_o)
-    store.start()
-    sent = msg.at[:, :, pl.ds(0, wide)]
-    pltpu.make_async_copy(sent, sent, sem_g).wait()
-    store.wait()
+                piece = f_in[f, block, :, pl.ds(starts[t], TILE)]
+                out[j, :, pl.ds(wide + f * narrow + t * TILE, TILE)] = piece.astype(BF)
+            return carry
+
+        lax.fori_loop(0, blocks, convert, 0, unroll=16)
+        flush(wide + f * narrow, narrow)
+    for store in stores:
+        store.wait()
 
 
 def pack(slots, grads, factors):
     steps, blocks, rows, side = grads.shape
-    narrow = 2 * (side - TILE)
+    shape = (blocks, rows, steps * side + 2 * (side - TILE))
     return pl.pallas_call(
         pack_body,
-        out_shape=jax.ShapeDtypeStruct((blocks, rows, steps * side + narrow), BF),
+        out_shape=jax.ShapeDtypeStruct(shape, BF),
         in_specs=[
             pl.BlockSpec(memory_space=pltpu.SMEM),
             pl.BlockSpec(memory_space=pl.ANY),
@@ -61,11 +70,12 @@
         ],
         out_specs=pl.BlockSpec(memory_space=pl.ANY),
         scratch_shapes=[
+            pltpu.VMEM(grads.shape, BF),
             pltpu.VMEM(factors.shape, F32),
-            pltpu.VMEM((blocks, rows, narrow), BF),
-            pltpu.SemaphoreType.DMA,
-            pltpu.SemaphoreType.DMA,
-            pltpu.SemaphoreType.DMA,
+            pltpu.VMEM(shape, BF),
+            pltpu.SemaphoreType.DMA((steps,)),
+            pltpu.SemaphoreType.DMA((2,)),
+            pltpu.SemaphoreType.DMA((steps + 2,)),
         ],
     )(slots, grads, factors)
 
@@ -171,15 +181,14 @@
     )(slots, layers, scales, got)
 
 
-def unpack_body(slots, got, update, sem):
+def unpack_body(slots, got, update):
     blocks = got.shape[0]
 
     def place(j, carry):
-        pltpu.make_async_copy(got.at[j], update.at[slots[j]], sem).start()
+        update[slots[j]] = got[j]
         return carry
 
-    lax.fori_loop(0, blocks, place, 0, unroll=8)
-    pltpu.make_async_copy(update, update, sem).wait()
+    lax.fori_loop(0, blocks, place, 0, unroll=16)
 
 
 def unpack(slots, got):
@@ -188,10 +197,9 @@
         out_shape=jax.ShapeDtypeStruct(got.shape, got.dtype),
         in_specs=[
             pl.BlockSpec(memory_space=pltpu.SMEM),
-            pl.BlockSpec(memory_space=pl.ANY),
-        ],
-        out_specs=pl.BlockSpec(memory_space=pl.ANY),
-        scratch_shapes=[pltpu.SemaphoreType.DMA],
+            pl.BlockSpec(memory_space=pltpu.VMEM),
+        ],
+        out_specs=pl.BlockSpec(memory_space=pltpu.VMEM),
     )(slots, got)
 
 

time: 150 us -> 88.9 us (0.59)
  Pallas kernels: 84.9 us -> 24 us
    pallas_call x1, Pallas kernels: 49.5 us -> 4.29 us  [pack(): pl.pallas_call(pack_body, out_shape=jax.ShapeDtypeStruct(shape, BF), in_s...]
    pallas_call x1, Pallas kernels: 17.7 us -> 2.02 us  [unpack(): pl.pallas_call(unpack_body, out_shape=jax.ShapeDtypeStruct(got.shape, got...]
where the time goes in v1:
time: 88.9 us; the launch traced here: 88.6 us
  blocking collectives  63.9 us (72%)
  Pallas kernels  24 us (27%)
    all_to_all x1, blocking collectives, body(): lax.all_to_all(message, axes, split_axis=0, concat_axis=0, tiled=True)  44.1 us
    all_to_all x1, blocking collectives, body(): lax.all_to_all(moved, axes, split_axis=0, concat_axis=0, tiled=True)  19.8 us
    pallas_call x1, Pallas kernels, compute(): pl.pallas_call(compute_body, out_shape=(jax.ShapeDtypeStruct((2, 1, side,...  17.7 us
    pallas_call x1, Pallas kernels, pack(): pl.pallas_call(pack_body, out_shape=jax.ShapeDtypeStruct(shape, BF), in_s...  4.29 us
    pallas_call x1, Pallas kernels, unpack(): pl.pallas_call(unpack_body, out_shape=jax.ShapeDtypeStruct(got.shape, got...  2.02 us

profile of v1, /device:TPU:1, one launch (start us, length us, event | category | flops | bytes accessed | tf_op | source)
XLA Modules:
  0.0 88.6 jit_solution(982856967521857814)
XLA Ops:
  0.6 4.3 %shard_map.68 = bf16[128,4,2304]{2,1,0:T(4,128)(2,1)} custom-call(s32[128]{0:T(128)} %slots.5, bf16[3,128,4,512]{3,2,1,0:T(4,128)(2,1)} %grads.1, f32[2,128,4,512]{3,2,1,0:T(4,128)} %factors.1), custom_call_target="tpu_custom_call" | custom-call | tf_op jit(solution)/shard_map/pallas_call | solution.py:63
  4.9 44.1 %all_to_all.10.got = bf16[128,4,2304]{2,1,0:T(4,128)(2,1)} all-to-all(bf16[128,4,2304]{2,1,0:T(4,128)(2,1)} %shard_map.68), channel_id=1, replica_groups=mesh['row'=8,'col'=16] {'row','col'}, dimensions={0} | all-to-all | bytes 4718592 | tf_op jit(solution)/shard_map/all_to_all | solution.py:209
  49.0 17.7 %shard_map.69 = (f32[2,1,512,512]{3,2,1,0:T(8,128)}, bf16[128,4,512]{2,1,0:T(4,128)(2,1)}) custom-call(s32[128]{0:T(128)} %slots.5, s32[128]{0:T(128)} %layers.1, f32[4]{0:T(128)} %scales.1, bf16[128,4,2304]{2,1,0:T(4,128)(2,1)} %all_to_all.10.got), custom_call_target="tpu_custom_call" | custom-call | tf_op jit(solution)/shard_map/pallas_call | solution.py:163
  66.8 19.8 %all_to_all.11.got = bf16[128,4,512]{2,1,0:T(4,128)(2,1)} all-to-all(bf16[128,4,512]{2,1,0:T(4,128)(2,1)} %get-tuple-element.5), channel_id=1, replica_groups=mesh['row'=8,'col'=16] {'row','col'}, dimensions={0} | all-to-all | bytes 1048576 | tf_op jit(solution)/shard_map/all_to_all | solution.py:213
  86.6 2.0 %shard_map.70 = bf16[128,4,512]{2,1,0:T(4,128)(2,1)} custom-call(s32[128]{0:T(128)} %slots.5, bf16[128,4,512]{2,1,0:T(4,128)(2,1)} %all_to_all.11.got), custom_call_target="tpu_custom_call" | custom-call | tf_op jit(solution)/shard_map/pallas_call | solution.py:195

commit v2 on v1

v2 whole, which is shorter than its diff:
```python
import jax
import jax.numpy as jnp
from jax import lax
from jax.experimental import pallas as pl
from jax.experimental.pallas import tpu as pltpu
from jax.sharding import PartitionSpec as P

ITERS = 6
TILE = 128
BF = jnp.bfloat16
F32 = jnp.float32


def pack_body(slots, grads, factors, msg, g_in, f_in, sem_g, sem_f):
    steps, blocks, rows, side = grads.shape
    wide = steps * side
    tiles = side // TILE
    narrow = (tiles - 1) * TILE
    loads = [pltpu.make_async_copy(grads.at[s], g_in.at[s], sem_g.at[s]) for s in range(steps)]
    loads += [pltpu.make_async_copy(factors.at[f], f_in.at[f], sem_f.at[f]) for f in range(2)]
    for load in loads:
        load.start()
    for s in range(steps):
        loads[s].wait()

        def gather(j, carry):
            msg[j, :, pl.ds(s * side, side)] = g_in[s, slots[j]]
            return carry

        lax.fori_loop(0, blocks, gather, 0, unroll=16)
    band = lax.axis_index("row") // 2
    starts = [pl.multiple_of(lax.rem(band + t, tiles) * TILE, TILE) for t in range(tiles - 1)]
    for f in range(2):
        loads[steps + f].wait()

        def convert(j, carry):
            block = slots[j]
            for t in range(tiles - 1):
                piece = f_in[f, block, :, pl.ds(starts[t], TILE)]
                msg[j, :, pl.ds(wide + f * narrow + t * TILE, TILE)] = piece.astype(BF)
            return carry

        lax.fori_loop(0, blocks, convert, 0, unroll=16)


def pack(slots, grads, factors):
    steps, blocks, rows, side = grads.shape
    shape = (blocks, rows, steps * side + 2 * (side - TILE))
    return pl.pallas_call(
        pack_body,
        out_shape=pltpu.VMEM(shape, BF),
        in_specs=[
            pl.BlockSpec(memory_space=pltpu.SMEM),
            pl.BlockSpec(memory_space=pl.ANY),
            pl.BlockSpec(memory_space=pl.ANY),
        ],
        out_specs=pl.BlockSpec(memory_space=pltpu.VMEM),
        scratch_shapes=[
            pltpu.VMEM(grads.shape, BF),
            pltpu.VMEM(factors.shape, F32),
            pltpu.SemaphoreType.DMA((steps,)),
            pltpu.SemaphoreType.DMA((2,)),
        ],
    )(slots, grads, factors)


def mm(a, b):
    return jnp.dot(a, b, preferred_element_type=F32)


def put(ref, f, top, low):
    half = low.shape[0]
    ref[f, :half, :] = top
    ref[f, half:, :half] = top[:, half:].T
    ref[f, half:, half:] = low


def symmetric_product(a_ref, b_ref, f):
    half = a_ref.shape[1] // 2
    top = mm(a_ref[f, :half, :], b_ref[f])
    low = mm(a_ref[f, half:, :], b_ref[f, :, half:])
    return top, low


def compute_body(
    slots, layers, scales, got, stats, update,
    raw, held, stat_ref, top_ref, low_ref, m_ref, x_ref, w_ref, g_ref, t_ref, sem, sem_in,
):
    sources, rows, _ = got.shape
    side = sources * rows
    half = side // 2
    tiles = side // TILE
    per = sources // tiles
    steps = g_ref.shape[0]
    loads = [
        pltpu.make_async_copy(got.at[:, :, pl.ds(s * side, side)], raw.at[s], sem_in.at[s])
        for s in range(steps)
    ]
    rest = pl.ds(steps * side, held.shape[2])
    loads.append(pltpu.make_async_copy(got.at[:, :, rest], held, sem_in.at[steps]))
    for load in loads:
        load.start()
    grams = [None, None]
    for s in range(steps):
        loads[s].wait()
        g_ref[s] = raw[s].reshape(side, side)
        t_ref[s] = g_ref[s].T
        pairs = ((g_ref, t_ref), (t_ref, g_ref))
        for f, (left, right) in enumerate(pairs):
            new = symmetric_product(left, right, s)
            grams[f] = new if s == 0 else tuple(a + b for a, b in zip(grams[f], new))
    loads[steps].wait()

    def block(f, i, t):
        lo = (f * (tiles - 1) + t) * TILE
        piece = held[i * per : (i + 1) * per, :, lo : lo + TILE]
        return piece.reshape(TILE, TILE).astype(F32)

    mid = tiles // 2
    for f in range(2):
        stat_ref[f, 0, :half, :] = grams[f][0] / side
        stat_ref[f, 0, half:, half:] = grams[f][1] / side
        for i in range(tiles):
            for k in range(tiles):
                if i >= mid and k < mid:
                    continue
                t = (k - i) % tiles
                piece = block(f, i, t) if t < tiles - 1 else block(f, k, 1).T
                a = slice(i * TILE, (i + 1) * TILE)
                c = slice(k * TILE, (k + 1) * TILE)
                stat_ref[f, 0, a, c] += piece
        stat_ref[f, 0, half:, :half] = stat_ref[f, 0, :half, half:].T
    out = pltpu.make_async_copy(stat_ref, stats, sem)
    out.start()
    eye = (
        lax.broadcasted_iota(jnp.int32, (half, half), 0)
        == lax.broadcasted_iota(jnp.int32, (half, half), 1)
    )
    unit = jnp.where(eye, 1.25, 0.0)
    wide_unit = jnp.concatenate([unit, jnp.zeros((half, half), F32)], axis=1)

    def total(x):
        return jnp.sum(jnp.sum(x * x, axis=0, keepdims=True), axis=1, keepdims=True)

    for f in range(2):
        top = stat_ref[f, 0, :half, :]
        low = stat_ref[f, 0, half:, half:]
        square = total(top) + total(top[:, half:]) + total(low)
        norm = jnp.sqrt(square)
        first = lax.rsqrt(jnp.sqrt(norm))
        top = top * (1.0 / norm)
        low = low * (1.0 / norm)
        top_ref[0, f] = top
        low_ref[0, f] = low
        put(m_ref, f, top.astype(BF), low.astype(BF))
        top = first * (wide_unit - 0.25 * top)
        low = first * (unit - 0.25 * low)
        top_ref[1, f] = top
        low_ref[1, f] = low
        put(x_ref, f, top.astype(BF), low.astype(BF))

    def move_x(f):
        top, low = symmetric_product(x_ref, m_ref, f)
        top = 1.25 * top_ref[1, f] - 0.25 * top
        low = 1.25 * low_ref[1, f] - 0.25 * low
        top_ref[1, f] = top
        low_ref[1, f] = low
        put(x_ref, f, top.astype(BF), low.astype(BF))

    def move_m():
        for f in range(2):
            top, low = symmetric_product(m_ref, m_ref, f)
            top = 0.0625 * top - 0.625 * top_ref[0, f]
            low = 0.0625 * low - 0.625 * low_ref[0, f]
            put(w_ref, f, top.astype(BF), low.astype(BF))
        for f in range(2):
            top, low = symmetric_product(w_ref, m_ref, f)
            top = 1.5625 * top_ref[0, f] + top
            low = 1.5625 * low_ref[0, f] + low
            top_ref[0, f] = top
            low_ref[0, f] = low
            put(m_ref, f, top.astype(BF), low.astype(BF))
        for f in range(2):
            top, low = symmetric_product(w_ref, m_ref, f)
            top = 1.5625 * top_ref[0, f] + top
            low = 1.5625 * low_ref[0, f] + low
            top_ref[0, f] = top
            low_ref[0, f] = low
            put(m_ref, f, top.astype(BF), low.astype(BF))

    move_m()

    def sweep(k, carry):
        for f in range(2):
            move_x(f)
        move_m()
        return carry

    lax.fori_loop(1, ITERS - 1, sweep, 0)
    for f in range(2):
        move_x(f)
    me = lax.axis_index("row") * lax.axis_size("col") + lax.axis_index("col")
    scale = scales[layers[slots[me]]]
    applied = mm(x_ref[0], g_ref[steps - 1]).astype(BF)
    result = (scale * mm(applied, x_ref[1])).astype(BF)
    update[...] = result.reshape(sources, rows, side)
    out.wait()


def compute(slots, layers, scales, got, steps):
    sources, rows, wide = got.shape
    side = sources * rows
    half = side // 2
    smem = pl.BlockSpec(memory_space=pltpu.SMEM)
    return pl.pallas_call(
        compute_body,
        out_shape=(
            jax.ShapeDtypeStruct((2, 1, side, side), F32),
            pltpu.VMEM((sources, rows, side), BF),
        ),
        in_specs=[smem, smem, smem, pl.BlockSpec(memory_space=pl.ANY)],
        out_specs=(
            pl.BlockSpec(memory_space=pl.ANY),
            pl.BlockSpec(memory_space=pltpu.VMEM),
        ),
        scratch_shapes=[
            pltpu.VMEM((steps, sources, rows, side), BF),
            pltpu.VMEM((sources, rows, wide - steps * side), BF),
            pltpu.VMEM((2, 1, side, side), F32),
            pltpu.VMEM((2, 2, half, side), F32),
            pltpu.VMEM((2, 2, half, half), F32),
            pltpu.VMEM((2, side, side), BF),
            pltpu.VMEM((2, side, side), BF),
            pltpu.VMEM((2, side, side), BF),
            pltpu.VMEM((steps, side, side), BF),
            pltpu.VMEM((steps, side, side), BF),
            pltpu.SemaphoreType.DMA,
            pltpu.SemaphoreType.DMA((steps + 1,)),
        ],
    )(slots, layers, scales, got)


def unpack_body(slots, got, update):
    blocks = got.shape[0]

    def place(j, carry):
        update[slots[j]] = got[j]
        return carry

    lax.fori_loop(0, blocks, place, 0, unroll=16)


def unpack(slots, got):
    return pl.pallas_call(
        unpack_body,
        out_shape=jax.ShapeDtypeStruct(got.shape, got.dtype),
        in_specs=[
            pl.BlockSpec(memory_space=pltpu.SMEM),
            pl.BlockSpec(memory_space=pltpu.VMEM),
        ],
        out_specs=pl.BlockSpec(memory_space=pltpu.VMEM),
    )(slots, got)


def body(gradients, factors, slot_block, layer_of_block, layer_step_scale):
    axes = ("row", "col")
    message = pack(slot_block, gradients, factors)
    owned = lax.all_to_all(message, axes, split_axis=0, concat_axis=0, tiled=True)
    new_factors, moved = compute(
        slot_block, layer_of_block, layer_step_scale, owned, gradients.shape[0]
    )
    returned = lax.all_to_all(moved, axes, split_axis=0, concat_axis=0, tiled=True)
    returned = pltpu.with_memory_space_constraint(returned, pltpu.VMEM)
    return (new_factors, unpack(slot_block, returned))


def solution(mesh):
    return jax.shard_map(
        body,
        mesh=mesh,
        in_specs=(
            P(None, None, ("row", "col"), None),
            P(None, None, ("row", "col"), None),
            P(),
            P(),
            P(),
        ),
        out_specs=(P(None, ("row", "col"), None, None), P(None, ("row", "col"), None)),
        check_vma=False,
    )
```

time: 88.9 us -> 83.3 us (0.937)
  Pallas kernels: 24 us -> 19.9 us
  blocking collectives: 63.9 us -> 62.5 us
    pallas_call x1, Pallas kernels: 17.7 us -> 14.8 us  [compute(): pl.pallas_call(compute_body, out_shape=(jax.ShapeDtypeStruct((2, 1, side,...]
    all_to_all x1, blocking collectives: 19.8 us -> 18.6 us  [body(): lax.all_to_all(moved, axes, split_axis=0, concat_axis=0, tiled=True)]
where the time goes in v2:
time: 83.3 us; the launch traced here: 83 us
  blocking collectives  62.5 us (75%)
  Pallas kernels  19.9 us (24%)
    all_to_all x1, blocking collectives, body(): lax.all_to_all(message, axes, split_axis=0, concat_axis=0, tiled=True)  43.9 us
    all_to_all x1, blocking collectives, body(): lax.all_to_all(moved, axes, split_axis=0, concat_axis=0, tiled=True)  18.6 us
    pallas_call x1, Pallas kernels, compute(): pl.pallas_call(compute_body, out_shape=(jax.ShapeDtypeStruct((2, 1, side,...  14.8 us
    pallas_call x1, Pallas kernels, pack(): pl.pallas_call(pack_body, out_shape=pltpu.VMEM(shape, BF), in_specs=[pl.B...  3.46 us

profile of v2, /device:TPU:1, one launch (start us, length us, event | category | flops | bytes accessed | tf_op | source)
XLA Modules:
  0.0 83.0 jit_solution(2039450803626840445)
XLA Ops:
  0.6 3.5 %shard_map.68 = bf16[128,4,2304]{2,1,0:T(4,128)(2,1)S(1)} custom-call(s32[128]{0:T(128)} %slots.5, bf16[3,128,4,512]{3,2,1,0:T(4,128)(2,1)} %grads.1, f32[2,128,4,512]{3,2,1,0:T(4,128)} %factors.1), custom_call_target="tpu_custom_call" | custom-call | tf_op jit(solution)/shard_map/pallas_call | solution.py:49
  4.1 43.9 %all_to_all.10.got = bf16[128,4,2304]{2,1,0:T(4,128)(2,1)} all-to-all(bf16[128,4,2304]{2,1,0:T(4,128)(2,1)S(1)} %shard_map.68), channel_id=1, replica_groups=mesh['row'=8,'col'=16] {'row','col'}, dimensions={0} | all-to-all | bytes 4718592 | tf_op jit(solution)/shard_map/all_to_all | solution.py:268
  48.0 14.8 %shard_map.69 = (f32[2,1,512,512]{3,2,1,0:T(8,128)}, bf16[128,4,512]{2,1,0:T(4,128)(2,1)S(1)}) custom-call(s32[128]{0:T(128)} %slots.5, s32[128]{0:T(128)} %layers.1, f32[4]{0:T(128)} %scales.1, bf16[128,4,2304]{2,1,0:T(4,128)(2,1)} %all_to_all.10.got), custom_call_target="tpu_custom_call" | custom-call | tf_op jit(solution)/shard_map/pallas_call | solution.py:215
  62.8 18.6 %all_to_all.11.got = bf16[128,4,512]{2,1,0:T(4,128)(2,1)S(1)} all-to-all(bf16[128,4,512]{2,1,0:T(4,128)(2,1)S(1)} %get-tuple-element.5), channel_id=1, replica_groups=mesh['row'=8,'col'=16] {'row','col'}, dimensions={0} | all-to-all | bytes 1048576 | tf_op jit(solution)/shard_map/all_to_all | solution.py:272
  81.4 1.6 %shard_map.70 = bf16[128,4,512]{2,1,0:T(4,128)(2,1)} custom-call(s32[128]{0:T(128)} %slots.5, bf16[128,4,512]{2,1,0:T(4,128)(2,1)S(1)} %all_to_all.11.got), custom_call_target="tpu_custom_call" | custom-call | tf_op jit(solution)/shard_map/pallas_call | solution.py:254

commit v3 on v2

--- a/solution.py
+++ b/solution.py
@@ -7,6 +7,7 @@
 
 ITERS = 6
 TILE = 128
+LIMIT = 32 * 1024 * 1024
 BF = jnp.bfloat16
 F32 = jnp.float32
 
@@ -61,6 +62,7 @@
             pltpu.SemaphoreType.DMA((steps,)),
             pltpu.SemaphoreType.DMA((2,)),
         ],
+        compiler_params=pltpu.CompilerParams(vmem_limit_bytes=LIMIT),
     )(slots, grads, factors)
 
 
@@ -84,7 +86,7 @@
 
 def compute_body(
     slots, layers, scales, got, stats, update,
-    raw, held, stat_ref, top_ref, low_ref, m_ref, x_ref, w_ref, g_ref, t_ref, sem, sem_in,
+    stat_ref, top_ref, low_ref, m_ref, x_ref, w_ref, g_ref, t_ref, sem,
 ):
     sources, rows, _ = got.shape
     side = sources * rows
@@ -92,34 +94,20 @@
     tiles = side // TILE
     per = sources // tiles
     steps = g_ref.shape[0]
-    loads = [
-        pltpu.make_async_copy(got.at[:, :, pl.ds(s * side, side)], raw.at[s], sem_in.at[s])
-        for s in range(steps)
-    ]
-    rest = pl.ds(steps * side, held.shape[2])
-    loads.append(pltpu.make_async_copy(got.at[:, :, rest], held, sem_in.at[steps]))
-    for load in loads:
-        load.start()
-    grams = [None, None]
+    mid = tiles // 2
+
+    def block(f, i, t):
+        lo = steps * side + (f * (tiles - 1) + t) * TILE
+        piece = got[i * per : (i + 1) * per, :, lo : lo + TILE]
+        return piece.reshape(TILE, TILE).astype(F32)
+
     for s in range(steps):
-        loads[s].wait()
-        g_ref[s] = raw[s].reshape(side, side)
+        g_ref[s] = got[:, :, s * side : (s + 1) * side].reshape(side, side)
         t_ref[s] = g_ref[s].T
-        pairs = ((g_ref, t_ref), (t_ref, g_ref))
-        for f, (left, right) in enumerate(pairs):
-            new = symmetric_product(left, right, s)
-            grams[f] = new if s == 0 else tuple(a + b for a, b in zip(grams[f], new))
-    loads[steps].wait()
-
-    def block(f, i, t):
-        lo = (f * (tiles - 1) + t) * TILE
-        piece = held[i * per : (i + 1) * per, :, lo : lo + TILE]
-        return piece.reshape(TILE, TILE).astype(F32)
-
-    mid = tiles // 2
-    for f in range(2):
-        stat_ref[f, 0, :half, :] = grams[f][0] / side
-        stat_ref[f, 0, half:, half:] = grams[f][1] / side
+    for f, (left, right) in enumerate(((g_ref, t_ref), (t_ref, g_ref))):
+        parts = [symmetric_product(left, right, s) for s in range(steps)]
+        top = sum(part[0] for part in parts[1:]) + parts[0][0]
+        low = sum(part[1] for part in parts[1:]) + parts[0][1]
         for i in range(tiles):
             for k in range(tiles):
                 if i >= mid and k < mid:
@@ -128,7 +116,12 @@
                 piece = block(f, i, t) if t < tiles - 1 else block(f, k, 1).T
                 a = slice(i * TILE, (i + 1) * TILE)
                 c = slice(k * TILE, (k + 1) * TILE)
-                stat_ref[f, 0, a, c] += piece
+                if i < mid:
+                    gram = top[a, c]
+                else:
+                    gram = low[(i - mid) * TILE : (i - mid + 1) * TILE, (k - mid) * TILE : (k - mid + 1) * TILE]
+                stat_ref[f, 0, a, c] = gram * (1.0 / side) + piece
+        put(m_ref, f, stat_ref[f, 0, :half, :].astype(BF), stat_ref[f, 0, half:, half:].astype(BF))
         stat_ref[f, 0, half:, :half] = stat_ref[f, 0, :half, half:].T
     out = pltpu.make_async_copy(stat_ref, stats, sem)
     out.start()
@@ -142,22 +135,44 @@
     def total(x):
         return jnp.sum(jnp.sum(x * x, axis=0, keepdims=True), axis=1, keepdims=True)
 
+    inverse = []
     for f in range(2):
         top = stat_ref[f, 0, :half, :]
         low = stat_ref[f, 0, half:, half:]
-        square = total(top) + total(top[:, half:]) + total(low)
-        norm = jnp.sqrt(square)
-        first = lax.rsqrt(jnp.sqrt(norm))
-        top = top * (1.0 / norm)
-        low = low * (1.0 / norm)
+        norm = jnp.sqrt(total(top) + total(top[:, half:]) + total(low))
+        inverse.append((1.0 / norm, lax.rsqrt(jnp.sqrt(norm))))
+    for f in range(2):
+        inv = inverse[f][0]
+        top, low = symmetric_product(m_ref, m_ref, f)
+        top = (0.0625 * top * inv - 0.625 * stat_ref[f, 0, :half, :]) * inv
+        low = (0.0625 * low * inv - 0.625 * stat_ref[f, 0, half:, half:]) * inv
+        put(w_ref, f, top.astype(BF), low.astype(BF))
+    for f in range(2):
+        inv, first = inverse[f]
+        stat_top = stat_ref[f, 0, :half, :]
+        stat_low = stat_ref[f, 0, half:, half:]
+        top, low = symmetric_product(w_ref, m_ref, f)
+        top = (1.5625 * stat_top + top) * inv
+        low = (1.5625 * stat_low + low) * inv
         top_ref[0, f] = top
         low_ref[0, f] = low
         put(m_ref, f, top.astype(BF), low.astype(BF))
-        top = first * (wide_unit - 0.25 * top)
-        low = first * (unit - 0.25 * low)
+        top = first * (wide_unit - (0.25 * inv) * stat_top)
+        low = first * (unit - (0.25 * inv) * stat_low)
         top_ref[1, f] = top
         low_ref[1, f] = low
         put(x_ref, f, top.astype(BF), low.astype(BF))
+
+    def last_m():
+        for f in range(2):
+            top, low = symmetric_product(w_ref, m_ref, f)
+            top = 1.5625 * top_ref[0, f] + top
+            low = 1.5625 * low_ref[0, f] + low
+            top_ref[0, f] = top
+            low_ref[0, f] = low
+            put(m_ref, f, top.astype(BF), low.astype(BF))
+
+    last_m()
 
     def move_x(f):
         top, low = symmetric_product(x_ref, m_ref, f)
@@ -173,22 +188,8 @@
             top = 0.0625 * top - 0.625 * top_ref[0, f]
             low = 0.0625 * low - 0.625 * low_ref[0, f]
             put(w_ref, f, top.astype(BF), low.astype(BF))
-        for f in range(2):
-            top, low = symmetric_product(w_ref, m_ref, f)
-            top = 1.5625 * top_ref[0, f] + top
-            low = 1.5625 * low_ref[0, f] + low
-            top_ref[0, f] = top
-            low_ref[0, f] = low
-            put(m_ref, f, top.astype(BF), low.astype(BF))
-        for f in range(2):
-            top, low = symmetric_product(w_ref, m_ref, f)
-            top = 1.5625 * top_ref[0, f] + top
-            low = 1.5625 * low_ref[0, f] + low
-            top_ref[0, f] = top
-            low_ref[0, f] = low
-            put(m_ref, f, top.astype(BF), low.astype(BF))
-
-    move_m()
+        last_m()
+        last_m()
 
     def sweep(k, carry):
         for f in range(2):
@@ -208,7 +209,7 @@
 
 
 def compute(slots, layers, scales, got, steps):
-    sources, rows, wide = got.shape
+    sources, rows, _ = got.shape
     side = sources * rows
     half = side // 2
     smem = pl.BlockSpec(memory_space=pltpu.SMEM)
@@ -218,14 +219,12 @@
             jax.ShapeDtypeStruct((2, 1, side, side), F32),
             pltpu.VMEM((sources, rows, side), BF),
         ),
-        in_specs=[smem, smem, smem, pl.BlockSpec(memory_space=pl.ANY)],
+        in_specs=[smem, smem, smem, pl.BlockSpec(memory_space=pltpu.VMEM)],
         out_specs=(
             pl.BlockSpec(memory_space=pl.ANY),
             pl.BlockSpec(memory_space=pltpu.VMEM),
         ),
         scratch_shapes=[
-            pltpu.VMEM((steps, sources, rows, side), BF),
-            pltpu.VMEM((sources, rows, wide - steps * side), BF),
             pltpu.VMEM((2, 1, side, side), F32),
             pltpu.VMEM((2, 2, half, side), F32),
             pltpu.VMEM((2, 2, half, half), F32),
@@ -235,8 +234,8 @@
             pltpu.VMEM((steps, side, side), BF),
             pltpu.VMEM((steps, side, side), BF),
             pltpu.SemaphoreType.DMA,
-            pltpu.SemaphoreType.DMA((steps + 1,)),
-        ],
+        ],
+        compiler_params=pltpu.CompilerParams(vmem_limit_bytes=LIMIT),
     )(slots, layers, scales, got)
 
 
@@ -259,13 +258,23 @@
             pl.BlockSpec(memory_space=pltpu.VMEM),
         ],
         out_specs=pl.BlockSpec(memory_space=pltpu.VMEM),
+        compiler_params=pltpu.CompilerParams(vmem_limit_bytes=LIMIT),
     )(slots, got)
+
+
+def in_hbm(x):
+    return pltpu.with_memory_space_constraint(x, pltpu.HBM)
 
 
 def body(gradients, factors, slot_block, layer_of_block, layer_step_scale):
     axes = ("row", "col")
+    tables = (slot_block, layer_of_block, layer_step_scale)
+    slot_block, layer_of_block, layer_step_scale = map(in_hbm, tables)
+    gradients = in_hbm(gradients)
+    factors = in_hbm(factors)
     message = pack(slot_block, gradients, factors)
     owned = lax.all_to_all(message, axes, split_axis=0, concat_axis=0, tiled=True)
+    owned = pltpu.with_memory_space_constraint(owned, pltpu.VMEM)
     new_factors, moved = compute(
         slot_block, layer_of_block, layer_step_scale, owned, gradients.shape[0]
     )

time: 83.3 us -> 81.3 us (0.976)
  Pallas kernels: 19.9 us -> 18.1 us
    pallas_call x1, Pallas kernels: 14.8 us -> 13 us  [compute(): pl.pallas_call(compute_body, out_shape=(jax.ShapeDtypeStruct((2, 1, side,...]
where the time goes in v3:
time: 81.3 us; the launch traced here: 81.1 us
  blocking collectives  62.4 us (77%)
  Pallas kernels  18.1 us (22%)
    all_to_all x1, blocking collectives, body(): lax.all_to_all(message, axes, split_axis=0, concat_axis=0, tiled=True)  43.8 us
    all_to_all x1, blocking collectives, body(): lax.all_to_all(moved, axes, split_axis=0, concat_axis=0, tiled=True)  18.6 us
    pallas_call x1, Pallas kernels, compute(): pl.pallas_call(compute_body, out_shape=(jax.ShapeDtypeStruct((2, 1, side,...  13 us
    pallas_call x1, Pallas kernels, pack(): pl.pallas_call(pack_body, out_shape=pltpu.VMEM(shape, BF), in_specs=[pl.B...  3.46 us
    pallas_call x1, Pallas kernels, unpack(): pl.pallas_call(unpack_body, out_shape=jax.ShapeDtypeStruct(got.shape, got...  1.63 us

profile of v3, /device:TPU:1, one launch (start us, length us, event | category | flops | bytes accessed | tf_op | source)
XLA Modules:
  0.0 81.1 jit_solution(3076325286196234509)
XLA Ops:
  0.6 3.5 %shard_map.68 = bf16[128,4,2304]{2,1,0:T(4,128)(2,1)S(1)} custom-call(s32[128]{0:T(128)} %slots.5, bf16[3,128,4,512]{3,2,1,0:T(4,128)(2,1)} %grads.1, f32[2,128,4,512]{3,2,1,0:T(4,128)} %factors.1), custom_call_target="tpu_custom_call" | custom-call | tf_op jit(solution)/shard_map/pallas_call | solution.py:50
  4.1 43.8 %all_to_all.10.got = bf16[128,4,2304]{2,1,0:T(4,128)(2,1)S(1)} all-to-all(bf16[128,4,2304]{2,1,0:T(4,128)(2,1)S(1)} %shard_map.68), channel_id=1, replica_groups=mesh['row'=8,'col'=16] {'row','col'}, dimensions={0} | all-to-all | bytes 4718592 | tf_op jit(solution)/shard_map/all_to_all | solution.py:276
  47.9 13.0 %shard_map.69 = (f32[2,1,512,512]{3,2,1,0:T(8,128)}, bf16[128,4,512]{2,1,0:T(4,128)(2,1)S(1)}) custom-call(s32[128]{0:T(128)} %slots.5, s32[128]{0:T(128)} %layers.1, f32[4]{0:T(128)} %scales.1, bf16[128,4,2304]{2,1,0:T(4,128)(2,1)S(1)} %all_to_all.10.got), custom_call_target="tpu_custom_call" | custom-call | tf_op jit(solution)/shard_map/pallas_call | solution.py:216
  60.9 18.6 %all_to_all.11.got = bf16[128,4,512]{2,1,0:T(4,128)(2,1)S(1)} all-to-all(bf16[128,4,512]{2,1,0:T(4,128)(2,1)S(1)} %get-tuple-element.5), channel_id=1, replica_groups=mesh['row'=8,'col'=16] {'row','col'}, dimensions={0} | all-to-all | bytes 1048576 | tf_op jit(solution)/shard_map/all_to_all | solution.py:281
  79.5 1.6 %shard_map.70 = bf16[128,4,512]{2,1,0:T(4,128)(2,1)} custom-call(s32[128]{0:T(128)} %slots.5, bf16[128,4,512]{2,1,0:T(4,128)(2,1)S(1)} %all_to_all.11.got), custom_call_target="tpu_custom_call" | custom-call | tf_op jit(solution)/shard_map/pallas_call | solution.py:253

commit v4 on v3

--- a/solution.py
+++ b/solution.py
@@ -7,20 +7,39 @@
 
 ITERS = 6
 TILE = 128
+CHUNKS = 4
 LIMIT = 32 * 1024 * 1024
 BF = jnp.bfloat16
 F32 = jnp.float32
 
 
-def pack_body(slots, grads, factors, msg, g_in, f_in, sem_g, sem_f):
+def pack_body(
+    slots_hbm, grads, factors, msg, places, slots, g_in, f_in, sem_s, sem_g, sem_f
+):
     steps, blocks, rows, side = grads.shape
     wide = steps * side
     tiles = side // TILE
-    narrow = (tiles - 1) * TILE
+    table = pltpu.make_async_copy(slots_hbm, slots, sem_s)
+    table.start()
+    band = lax.axis_index("row")
+    odd = lax.rem(band, 2)
+    picks = (2 * odd, 1, 2 - 2 * odd)
+    tile_loads = []
+    for f in range(2):
+        for t, pick in enumerate(picks):
+            start = pl.multiple_of(lax.rem(band // 2 + pick, tiles) * TILE, TILE)
+            tile = factors.at[f, :, :, pl.ds(start, TILE)]
+            tile_loads.append(pltpu.make_async_copy(tile, f_in.at[f, t], sem_f.at[f, t]))
     loads = [pltpu.make_async_copy(grads.at[s], g_in.at[s], sem_g.at[s]) for s in range(steps)]
-    loads += [pltpu.make_async_copy(factors.at[f], f_in.at[f], sem_f.at[f]) for f in range(2)]
-    for load in loads:
+    for load in loads + tile_loads:
         load.start()
+    table.wait()
+
+    def invert(j, carry):
+        places[slots[j]] = j
+        return carry
+
+    lax.fori_loop(0, blocks, invert, 0, unroll=16)
     for s in range(steps):
         loads[s].wait()
 
@@ -29,38 +48,47 @@
             return carry
 
         lax.fori_loop(0, blocks, gather, 0, unroll=16)
-    band = lax.axis_index("row") // 2
-    starts = [pl.multiple_of(lax.rem(band + t, tiles) * TILE, TILE) for t in range(tiles - 1)]
-    for f in range(2):
-        loads[steps + f].wait()
-
-        def convert(j, carry):
-            block = slots[j]
-            for t in range(tiles - 1):
-                piece = f_in[f, block, :, pl.ds(starts[t], TILE)]
-                msg[j, :, pl.ds(wide + f * narrow + t * TILE, TILE)] = piece.astype(BF)
-            return carry
-
-        lax.fori_loop(0, blocks, convert, 0, unroll=16)
+    for load in tile_loads:
+        load.wait()
+    lane = lax.broadcasted_iota(jnp.int32, (rows, TILE), 1)
+    mine = (lane // (TILE // 2)) == odd
+
+    def convert(j, carry):
+        block = slots[j]
+        for f in range(2):
+            for t in range(2):
+                lo = wide + (2 * f + t) * TILE
+                msg[j, :, pl.ds(lo, TILE)] = f_in[f, t, block].astype(BF)
+        other = pltpu.roll(f_in[1, 2, block], TILE // 2, 1)
+        shared = jnp.where(mine, f_in[0, 2, block], other)
+        msg[j, :, pl.ds(wide + 4 * TILE, TILE)] = shared.astype(BF)
+        return carry
+
+    lax.fori_loop(0, blocks, convert, 0, unroll=16)
 
 
 def pack(slots, grads, factors):
     steps, blocks, rows, side = grads.shape
-    shape = (blocks, rows, steps * side + 2 * (side - TILE))
+    shape = (blocks, rows, steps * side + 5 * TILE)
+    anywhere = pl.BlockSpec(memory_space=pl.ANY)
     return pl.pallas_call(
         pack_body,
-        out_shape=pltpu.VMEM(shape, BF),
-        in_specs=[
+        out_shape=(
+            pltpu.VMEM(shape, BF),
+            jax.ShapeDtypeStruct(slots.shape, jnp.int32),
+        ),
+        in_specs=[anywhere, anywhere, anywhere],
+        out_specs=(
+            pl.BlockSpec(memory_space=pltpu.VMEM),
             pl.BlockSpec(memory_space=pltpu.SMEM),
-            pl.BlockSpec(memory_space=pl.ANY),
-            pl.BlockSpec(memory_space=pl.ANY),
-        ],
-        out_specs=pl.BlockSpec(memory_space=pltpu.VMEM),
+        ),
         scratch_shapes=[
+            pltpu.SMEM(slots.shape, jnp.int32),
             pltpu.VMEM(grads.shape, BF),
-            pltpu.VMEM(factors.shape, F32),
+            pltpu.VMEM((2, 3, blocks, rows, TILE), F32),
+            pltpu.SemaphoreType.DMA,
             pltpu.SemaphoreType.DMA((steps,)),
-            pltpu.SemaphoreType.DMA((2,)),
+            pltpu.SemaphoreType.DMA((2, 3)),
         ],
         compiler_params=pltpu.CompilerParams(vmem_limit_bytes=LIMIT),
     )(slots, grads, factors)
@@ -79,9 +107,9 @@
 
 def symmetric_product(a_ref, b_ref, f):
     half = a_ref.shape[1] // 2
-    top = mm(a_ref[f, :half, :], b_ref[f])
-    low = mm(a_ref[f, half:, :], b_ref[f, :, half:])
-    return top, low
+    right = mm(a_ref[f], b_ref[f, :, half:])
+    left = mm(a_ref[f, :half, :], b_ref[f, :, :half])
+    return jnp.concatenate([left, right[:half]], axis=1), right[half:]
 
 
 def compute_body(
@@ -96,10 +124,43 @@
     steps = g_ref.shape[0]
     mid = tiles // 2
 
-    def block(f, i, t):
-        lo = steps * side + (f * (tiles - 1) + t) * TILE
-        piece = got[i * per : (i + 1) * per, :, lo : lo + TILE]
-        return piece.reshape(TILE, TILE).astype(F32)
+    band = per // 2
+    base = steps * side
+
+    def rows_of(i, parity, lo):
+        first = i * per + parity * band
+        piece = got[first : first + band, :, base + lo : base + lo + TILE]
+        return piece.reshape(TILE // 2, TILE).astype(F32)
+
+    def halves(f, i, parity):
+        piece = rows_of(i, parity, 4 * TILE)
+        return pltpu.roll(piece, TILE // 2, 1) if f else piece
+
+    def own(f, i, parity, t):
+        return rows_of(i, parity, (2 * f + t) * TILE)
+
+    def near(f, i):
+        return jnp.concatenate([own(f, i, 0, 0), halves(f, i, 1)], axis=0)
+
+    def next_to(f, i):
+        return jnp.concatenate([own(f, i, 0, 1), own(f, i, 1, 1)], axis=0)
+
+    def far(f, i):
+        return jnp.concatenate([halves(f, i, 0), own(f, i, 1, 0)], axis=0)
+
+    upper_row = lax.broadcasted_iota(jnp.int32, (TILE, TILE), 0) < TILE // 2
+    upper_col = lax.broadcasted_iota(jnp.int32, (TILE, TILE), 1) < TILE // 2
+
+    def block(f, i, k):
+        t = (k - i) % tiles
+        if t == 0:
+            piece = near(f, i)
+            return jnp.where(jnp.logical_or(upper_row, ~upper_col), piece, piece.T)
+        if t == 1:
+            return next_to(f, i)
+        if t == 2:
+            return jnp.where(jnp.logical_or(~upper_row, upper_col), far(f, i), far(f, k).T)
+        return next_to(f, k).T
 
     for s in range(steps):
         g_ref[s] = got[:, :, s * side : (s + 1) * side].reshape(side, side)
@@ -112,8 +173,7 @@
             for k in range(tiles):
                 if i >= mid and k < mid:
                     continue
-                t = (k - i) % tiles
-                piece = block(f, i, t) if t < tiles - 1 else block(f, k, 1).T
+                piece = block(f, i, k)
                 a = slice(i * TILE, (i + 1) * TILE)
                 c = slice(k * TILE, (k + 1) * TILE)
                 if i < mid:
@@ -239,17 +299,25 @@
     )(slots, layers, scales, got)
 
 
-def unpack_body(slots, got, update):
+def unpack_body(places, got, update, ordered, sem):
     blocks = got.shape[0]
-
-    def place(j, carry):
-        update[slots[j]] = got[j]
-        return carry
-
-    lax.fori_loop(0, blocks, place, 0, unroll=16)
-
-
-def unpack(slots, got):
+    chunk = blocks // CHUNKS
+    stores = []
+    for c in range(CHUNKS):
+
+        def place(j, carry):
+            ordered[j] = got[places[j]]
+            return carry
+
+        lax.fori_loop(c * chunk, (c + 1) * chunk, place, 0, unroll=16)
+        span = pl.ds(c * chunk, chunk)
+        stores.append(pltpu.make_async_copy(ordered.at[span], update.at[span], sem.at[c]))
+        stores[c].start()
+    for store in stores:
+        store.wait()
+
+
+def unpack(places, got):
     return pl.pallas_call(
         unpack_body,
         out_shape=jax.ShapeDtypeStruct(got.shape, got.dtype),
@@ -257,9 +325,10 @@
             pl.BlockSpec(memory_space=pltpu.SMEM),
             pl.BlockSpec(memory_space=pltpu.VMEM),
         ],
-        out_specs=pl.BlockSpec(memory_space=pltpu.VMEM),
+        out_specs=pl.BlockSpec(memory_space=pl.ANY),
+        scratch_shapes=[pltpu.VMEM(got.shape, got.dtype), pltpu.SemaphoreType.DMA((CHUNKS,))],
         compiler_params=pltpu.CompilerParams(vmem_limit_bytes=LIMIT),
-    )(slots, got)
+    )(places, got)
 
 
 def in_hbm(x):
@@ -272,7 +341,7 @@
     slot_block, layer_of_block, layer_step_scale = map(in_hbm, tables)
     gradients = in_hbm(gradients)
     factors = in_hbm(factors)
-    message = pack(slot_block, gradients, factors)
+    message, places = pack(slot_block, gradients, factors)
     owned = lax.all_to_all(message, axes, split_axis=0, concat_axis=0, tiled=True)
     owned = pltpu.with_memory_space_constraint(owned, pltpu.VMEM)
     new_factors, moved = compute(
@@ -280,7 +349,7 @@
     )
     returned = lax.all_to_all(moved, axes, split_axis=0, concat_axis=0, tiled=True)
     returned = pltpu.with_memory_space_constraint(returned, pltpu.VMEM)
-    return (new_factors, unpack(slot_block, returned))
+    return (new_factors, unpack(places, returned))
 
 
 def solution(mesh):

time: 81.3 us -> 79.3 us (0.975)
  blocking collectives: 62.4 us -> 60.9 us
    all_to_all x1, blocking collectives: 43.8 us -> 42.4 us  [body(): lax.all_to_all(message, axes, split_axis=0, concat_axis=0, tiled=True)]
where the time goes in v4:
time: 79.3 us; the launch traced here: 79.1 us
  blocking collectives  60.9 us (77%)
  Pallas kernels  17.5 us (22%)
    all_to_all x1, blocking collectives, body(): lax.all_to_all(message, axes, split_axis=0, concat_axis=0, tiled=True)  42.4 us
    all_to_all x1, blocking collectives, body(): lax.all_to_all(moved, axes, split_axis=0, concat_axis=0, tiled=True)  18.6 us
    pallas_call x1, Pallas kernels, compute(): pl.pallas_call(compute_body, out_shape=(jax.ShapeDtypeStruct((2, 1, side,...  12.6 us
    pallas_call x1, Pallas kernels, pack(): pl.pallas_call(pack_body, out_shape=(pltpu.VMEM(shape, BF), jax.ShapeDtyp...  3.48 us

profile of v4, /device:TPU:1, one launch (start us, length us, event | category | flops | bytes accessed | tf_op | source)
XLA Modules:
  0.0 79.1 jit_solution(11286888491106674618)
XLA Ops:
  0.6 3.5 %shard_map.68 = (bf16[128,4,2176]{2,1,0:T(4,128)(2,1)S(1)}, s32[128]{0:T(128)S(1)}) custom-call(s32[128]{0:T(128)} %slots.1, bf16[3,128,4,512]{3,2,1,0:T(4,128)(2,1)} %grads.1, f32[2,128,4,512]{3,2,1,0:T(4,128)} %factors.1), custom_call_target="tpu_custom_call" | custom-call | tf_op jit(solution)/shard_map/pallas_call | solution.py:74
  4.1 42.4 %all_to_all.10.got = bf16[128,4,2176]{2,1,0:T(4,128)(2,1)S(1)} all-to-all(bf16[128,4,2176]{2,1,0:T(4,128)(2,1)S(1)} %get-tuple-element.6), channel_id=1, replica_groups=mesh['row'=8,'col'=16] {'row','col'}, dimensions={0} | all-to-all | bytes 4456448 | tf_op jit(solution)/shard_map/all_to_all | solution.py:345
  46.5 12.6 %shard_map.69 = (f32[2,1,512,512]{3,2,1,0:T(8,128)}, bf16[128,4,512]{2,1,0:T(4,128)(2,1)S(1)}) custom-call(s32[128]{0:T(128)} %slots.1, s32[128]{0:T(128)} %layers.1, f32[4]{0:T(128)} %scales.1, bf16[128,4,2176]{2,1,0:T(4,128)(2,1)S(1)} %all_to_all.10.got), custom_call_target="tpu_custom_call" | custom-call | tf_op jit(solution)/shard_map/pallas_call | solution.py:276
  59.1 18.6 %all_to_all.11.got = bf16[128,4,512]{2,1,0:T(4,128)(2,1)S(1)} all-to-all(bf16[128,4,512]{2,1,0:T(4,128)(2,1)S(1)} %get-tuple-element.9), channel_id=1, replica_groups=mesh['row'=8,'col'=16] {'row','col'}, dimensions={0} | all-to-all | bytes 1048576 | tf_op jit(solution)/shard_map/all_to_all | solution.py:350
  77.7 1.4 %shard_map.70 = bf16[128,4,512]{2,1,0:T(4,128)(2,1)} custom-call(s32[128]{0:T(128)S(1)} %get-tuple-element.8.places, bf16[128,4,512]{2,1,0:T(4,128)(2,1)S(1)} %all_to_all.11.got), custom_call_target="tpu_custom_call" | custom-call | tf_op jit(solution)/shard_map/pallas_call | solution.py:321

commit v5 on v4

--- a/solution.py
+++ b/solution.py
@@ -47,7 +47,7 @@
             msg[j, :, pl.ds(s * side, side)] = g_in[s, slots[j]]
             return carry
 
-        lax.fori_loop(0, blocks, gather, 0, unroll=16)
+        lax.fori_loop(0, blocks, gather, 0, unroll=64)
     for load in tile_loads:
         load.wait()
     lane = lax.broadcasted_iota(jnp.int32, (rows, TILE), 1)
@@ -64,7 +64,7 @@
         msg[j, :, pl.ds(wide + 4 * TILE, TILE)] = shared.astype(BF)
         return carry
 
-    lax.fori_loop(0, blocks, convert, 0, unroll=16)
+    lax.fori_loop(0, blocks, convert, 0, unroll=128)
 
 
 def pack(slots, grads, factors):
@@ -309,7 +309,7 @@
             ordered[j] = got[places[j]]
             return carry
 
-        lax.fori_loop(c * chunk, (c + 1) * chunk, place, 0, unroll=16)
+        lax.fori_loop(c * chunk, (c + 1) * chunk, place, 0, unroll=32)
         span = pl.ds(c * chunk, chunk)
         stores.append(pltpu.make_async_copy(ordered.at[span], update.at[span], sem.at[c]))
         stores[c].start()

time: 79.3 us -> 78.8 us (level)
  no operation moved by 1% of the time
where the time goes in v5:
time: 78.8 us; the launch traced here: 78.6 us
  blocking collectives  60.9 us (77%)
  Pallas kernels  17 us (22%)
    all_to_all x1, blocking collectives, body(): lax.all_to_all(message, axes, split_axis=0, concat_axis=0, tiled=True)  42.4 us
    all_to_all x1, blocking collectives, body(): lax.all_to_all(moved, axes, split_axis=0, concat_axis=0, tiled=True)  18.5 us
    pallas_call x1, Pallas kernels, compute(): pl.pallas_call(compute_body, out_shape=(jax.ShapeDtypeStruct((2, 1, side,...  12.6 us
    pallas_call x1, Pallas kernels, pack(): pl.pallas_call(pack_body, out_shape=(pltpu.VMEM(shape, BF), jax.ShapeDtyp...  3 us

profile of v5, /device:TPU:1, one launch (start us, length us, event | category | flops | bytes accessed | tf_op | source)
XLA Modules:
  0.0 78.6 jit_solution(13843216703698524307)
XLA Ops:
  0.6 3.0 %shard_map.68 = (bf16[128,4,2176]{2,1,0:T(4,128)(2,1)S(1)}, s32[128]{0:T(128)S(1)}) custom-call(s32[128]{0:T(128)} %slots.1, bf16[3,128,4,512]{3,2,1,0:T(4,128)(2,1)} %grads.1, f32[2,128,4,512]{3,2,1,0:T(4,128)} %factors.1), custom_call_target="tpu_custom_call" | custom-call | tf_op jit(solution)/shard_map/pallas_call | solution.py:74
  3.6 42.4 %all_to_all.10.got = bf16[128,4,2176]{2,1,0:T(4,128)(2,1)S(1)} all-to-all(bf16[128,4,2176]{2,1,0:T(4,128)(2,1)S(1)} %get-tuple-element.6), channel_id=1, replica_groups=mesh['row'=8,'col'=16] {'row','col'}, dimensions={0} | all-to-all | bytes 4456448 | tf_op jit(solution)/shard_map/all_to_all | solution.py:345
  46.0 12.6 %shard_map.69 = (f32[2,1,512,512]{3,2,1,0:T(8,128)}, bf16[128,4,512]{2,1,0:T(4,128)(2,1)S(1)}) custom-call(s32[128]{0:T(128)} %slots.1, s32[128]{0:T(128)} %layers.1, f32[4]{0:T(128)} %scales.1, bf16[128,4,2176]{2,1,0:T(4,128)(2,1)S(1)} %all_to_all.10.got), custom_call_target="tpu_custom_call" | custom-call | tf_op jit(solution)/shard_map/pallas_call | solution.py:276
  58.7 18.5 %all_to_all.11.got = bf16[128,4,512]{2,1,0:T(4,128)(2,1)S(1)} all-to-all(bf16[128,4,512]{2,1,0:T(4,128)(2,1)S(1)} %get-tuple-element.9), channel_id=1, replica_groups=mesh['row'=8,'col'=16] {'row','col'}, dimensions={0} | all-to-all | bytes 1048576 | tf_op jit(solution)/shard_map/all_to_all | solution.py:350
  77.2 1.4 %shard_map.70 = bf16[128,4,512]{2,1,0:T(4,128)(2,1)} custom-call(s32[128]{0:T(128)S(1)} %get-tuple-element.8.places, bf16[128,4,512]{2,1,0:T(4,128)(2,1)S(1)} %all_to_all.11.got), custom_call_target="tpu_custom_call" | custom-call | tf_op jit(solution)/shard_map/pallas_call | solution.py:321

commit v6 on v5

--- a/solution.py
+++ b/solution.py
@@ -48,23 +48,24 @@
             return carry
 
         lax.fori_loop(0, blocks, gather, 0, unroll=64)
-    for load in tile_loads:
-        load.wait()
     lane = lax.broadcasted_iota(jnp.int32, (rows, TILE), 1)
     mine = (lane // (TILE // 2)) == odd
-
-    def convert(j, carry):
-        block = slots[j]
-        for f in range(2):
+    for f in range(2):
+        for load in tile_loads[3 * f : 3 * f + 3]:
+            load.wait()
+
+        def convert(j, carry):
+            block = slots[j]
             for t in range(2):
                 lo = wide + (2 * f + t) * TILE
                 msg[j, :, pl.ds(lo, TILE)] = f_in[f, t, block].astype(BF)
-        other = pltpu.roll(f_in[1, 2, block], TILE // 2, 1)
-        shared = jnp.where(mine, f_in[0, 2, block], other)
-        msg[j, :, pl.ds(wide + 4 * TILE, TILE)] = shared.astype(BF)
-        return carry
-
-    lax.fori_loop(0, blocks, convert, 0, unroll=128)
+            if f:
+                other = pltpu.roll(f_in[1, 2, block], TILE // 2, 1)
+                shared = jnp.where(mine, f_in[0, 2, block], other)
+                msg[j, :, pl.ds(wide + 4 * TILE, TILE)] = shared.astype(BF)
+            return carry
+
+        lax.fori_loop(0, blocks, convert, 0, unroll=128)
 
 
 def pack(slots, grads, factors):

time: 78.8 us -> 78.8 us (level)
  no operation moved by 1% of the time
where the time goes in v6:
time: 78.8 us; the launch traced here: 78.6 us
  blocking collectives  60.9 us (77%)
  Pallas kernels  17 us (22%)
    all_to_all x1, blocking collectives, body(): lax.all_to_all(message, axes, split_axis=0, concat_axis=0, tiled=True)  42.4 us
    all_to_all x1, blocking collectives, body(): lax.all_to_all(moved, axes, split_axis=0, concat_axis=0, tiled=True)  18.6 us
    pallas_call x1, Pallas kernels, compute(): pl.pallas_call(compute_body, out_shape=(jax.ShapeDtypeStruct((2, 1, side,...  12.6 us
    pallas_call x1, Pallas kernels, pack(): pl.pallas_call(pack_body, out_shape=(pltpu.VMEM(shape, BF), jax.ShapeDtyp...  3.01 us

profile of v6, /device:TPU:1, one launch (start us, length us, event | category | flops | bytes accessed | tf_op | source)
XLA Modules:
  0.0 78.6 jit_solution(8847282401174635694)
XLA Ops:
  0.6 3.0 %shard_map.68 = (bf16[128,4,2176]{2,1,0:T(4,128)(2,1)S(1)}, s32[128]{0:T(128)S(1)}) custom-call(s32[128]{0:T(128)} %slots.1, bf16[3,128,4,512]{3,2,1,0:T(4,128)(2,1)} %grads.1, f32[2,128,4,512]{3,2,1,0:T(4,128)} %factors.1), custom_call_target="tpu_custom_call" | custom-call | tf_op jit(solution)/shard_map/pallas_call | solution.py:75
  3.6 42.4 %all_to_all.10.got = bf16[128,4,2176]{2,1,0:T(4,128)(2,1)S(1)} all-to-all(bf16[128,4,2176]{2,1,0:T(4,128)(2,1)S(1)} %get-tuple-element.6), channel_id=1, replica_groups=mesh['row'=8,'col'=16] {'row','col'}, dimensions={0} | all-to-all | bytes 4456448 | tf_op jit(solution)/shard_map/all_to_all | solution.py:346
  46.0 12.6 %shard_map.69 = (f32[2,1,512,512]{3,2,1,0:T(8,128)}, bf16[128,4,512]{2,1,0:T(4,128)(2,1)S(1)}) custom-call(s32[128]{0:T(128)} %slots.1, s32[128]{0:T(128)} %layers.1, f32[4]{0:T(128)} %scales.1, bf16[128,4,2176]{2,1,0:T(4,128)(2,1)S(1)} %all_to_all.10.got), custom_call_target="tpu_custom_call" | custom-call | tf_op jit(solution)/shard_map/pallas_call | solution.py:277
  58.7 18.6 %all_to_all.11.got = bf16[128,4,512]{2,1,0:T(4,128)(2,1)S(1)} all-to-all(bf16[128,4,512]{2,1,0:T(4,128)(2,1)S(1)} %get-tuple-element.9), channel_id=1, replica_groups=mesh['row'=8,'col'=16] {'row','col'}, dimensions={0} | all-to-all | bytes 1048576 | tf_op jit(solution)/shard_map/all_to_all | solution.py:351
  77.2 1.4 %shard_map.70 = bf16[128,4,512]{2,1,0:T(4,128)(2,1)} custom-call(s32[128]{0:T(128)S(1)} %get-tuple-element.8.places, bf16[128,4,512]{2,1,0:T(4,128)(2,1)S(1)} %all_to_all.11.got), custom_call_target="tpu_custom_call" | custom-call | tf_op jit(solution)/shard_map/pallas_call | solution.py:322
